TPU v7x, 256 devices: a whole 4x4x8 slice. The times are simulated.
256 devices in a mesh: seq: 32 (over z, x_lo, core), head: 8 (over y, x_hi).
Axes of the slice: x: 4 (x_hi: 2, x_lo: 2; x = x_hi * 2 + x_lo), y: 4, z: 8, core: 2. Of those that a mesh axis runs over, the one named last changes fastest.
Arguments:
- queries: bfloat16 [12288, 8192], P('seq', 'head'), may hold values from -6 to 6
- keys: bfloat16 [12288, 1024], P('seq', 'head'), may hold values from -6 to 6
- values: bfloat16 [12288, 1024], P('seq', 'head'), may hold values from -6 to 6
- windows: int32 [8], P('head'), may hold values from 256 to 4096, as said below
- out_weight: bfloat16 [8192, 8192], P('head', 'seq'), may hold values from -0.0625 to 0.0625
Outputs:
- projected: bfloat16 [12288, 8192], P('seq', 'head')
Inputs may be any that keep to these rules, and one draw needn't show every extreme that they name: `windows`: every window is a multiple of 128; in every draw some group has exactly 4096, and where there are three groups or more another has exactly 256.
All inputs are finite; a program needn't handle non-finite values.
Results may differ from a plain program's by a relative error of at most 0.014.
Values may be sent and summed in bfloat16 or wider, within the bound.
A program may use at most 128 MiB of HBM per device.

v0:
```python
import math

import jax
import jax.numpy as jnp
from jax import lax
from jax.sharding import PartitionSpec as P

DH = 128
QPG = 8
WMAX = 4096


def passed_along(block, axis, distance):
    devices = range(lax.axis_size(axis))
    route = [(i - distance, i) for i in devices if i - distance in devices]
    return lax.ppermute(block, axis, route)


def body(queries, keys, values, windows, out_weight):
    tok_rows = queries.shape[0]
    groups = keys.shape[1] // DH
    score_scale = 1.0 / math.sqrt(DH)
    start_pos = lax.axis_index("seq") * tok_rows
    query_row_matrix = (
        queries.reshape(tok_rows, groups, QPG, DH)
        .transpose(1, 2, 0, 3)
        .reshape(groups, QPG * tok_rows, DH)
    )
    pair = jnp.stack([keys.reshape(tok_rows, groups, DH), values.reshape(tok_rows, groups, DH)])
    query_pos = start_pos + jnp.arange(QPG * tok_rows, dtype=jnp.int32) % tok_rows
    halo_blocks = (WMAX + tok_rows - 2) // tok_rows

    def attend(running, query_key_block_couple, key_start):
        top_now, total, accum = running
        scores = (
            jnp.einsum(
                "yzf,wyf->yzw",
                query_row_matrix,
                query_key_block_couple[0],
                preferred_element_type=jnp.float32,
            )
            * score_scale
        )
        key_pos = key_start + jnp.arange(tok_rows, dtype=jnp.int32)
        allowed = (
            (key_pos[None, None, :] <= query_pos[None, :, None])
            & (key_pos[None, None, :] > query_pos[None, :, None] - windows[:, None, None])
            & (key_pos[None, None, :] >= 0)
        )
        block_top = jnp.max(jnp.where(allowed, scores, -1e30), axis=2)
        fresh_peak_score = jnp.maximum(top_now, block_top)
        weights = jnp.where(allowed, jnp.exp(scores - fresh_peak_score[:, :, None]), 0.0)
        rescale = jnp.exp(top_now - fresh_peak_score)
        total = total * rescale + jnp.sum(weights, axis=2)
        accum = accum * rescale[:, :, None] + jnp.einsum(
            "qki,iqx->qkx",
            weights.astype(jnp.bfloat16),
            query_key_block_couple[1],
            preferred_element_type=jnp.float32,
        )
        return (fresh_peak_score, total, accum)

    def maybe_attend(running, query_key_block_couple, key_start):
        return attend(running, query_key_block_couple, key_start)

    initial = (
        jnp.full((groups, QPG * tok_rows), -1e30, jnp.float32),
        jnp.zeros((groups, QPG * tok_rows), jnp.float32),
        jnp.zeros((groups, QPG * tok_rows, DH), jnp.float32),
    )
    running = attend(initial, pair, start_pos)

    def forward_turn(step_index, carry):
        current, moving = carry
        moving = passed_along(moving, "seq", 1)
        current = maybe_attend(current, moving, start_pos - step_index * tok_rows)
        return (current, moving)

    running, moving = lax.fori_loop(1, halo_blocks + 1, forward_turn, (running, pair))
    top_now, total, accum = running
    attended = (accum / total[:, :, None]).astype(jnp.bfloat16)
    attended = (
        attended.reshape(groups, QPG, tok_rows, DH)
        .transpose(2, 0, 1, 3)
        .reshape(tok_rows, groups * QPG * DH)
    )
    partial_sums = jnp.dot(
        attended,
        lax.all_gather(out_weight, "seq", axis=1, tiled=True),
        preferred_element_type=jnp.float32,
    )
    return lax.psum_scatter(
        partial_sums.astype(jnp.bfloat16), "head", scatter_dimension=1, tiled=True
    )


def solution(mesh):
    placed = (P("seq", "head"), P("seq", "head"), P("seq", "head"), P("head"), P("head", "seq"))
    return jax.shard_map(
        body, mesh=mesh, in_specs=placed, out_specs=P("seq", "head"), check_vma=False
    )
```

profile of v0, /device:TPU:3, one launch (start us, length us, event | category | flops | bytes accessed | tf_op | source)
XLA Modules:
  0.0 333.2 jit_solution(14402265725980212379)
XLA Ops:
  10.4 2.5 select_reduce_fusion.1
  14.9 2.2 fusion.14
  17.1 168.9 %while.21 = (s32[]{:T(128)}, f32[1,3072]{1,0:T(1,128)S(1)}, f32[1,3072]{1,0:T(1,128)S(1)}, f32[1,3072,128]{2,1,0:T(8,128)S(1)}, bf16[2,384,1,128]{3,1,2,0:T(8,12...) while((s32[]{:T(128)}, f32[1,3072]{1,0:T(1,128)S(1)}, ...), condition=%wide.region_5.6_spmd.clone.clone, body=%wide.region_2.5_spmd.clone.clone.sunk | while | flops 629570688 | bytes 19768244 | solution.py:79
  17.1 4.1 %collective-permute-start = (bf16[2,384,1,128]{3,1,2,0:T(8,128)(2,1)S(1)}, bf16[2,384,1,128]{3,1,2,0:T(8,128)(2,1)S(1)}, u32[]{:S(2)}, u32[]{:S(2)}) collective-permute-start(bf16[2,384,1,128]{3,1,2,0:T(8,128)(2,1)S(1)} %get-tuple-element.306), channel_id=1, source_target_pairs={{0,8},{8,16},{16,24},{24,32},{32,40},{40,48},{48,56},{56,64},{64,7... | collective-permute-start | bytes 589832 | tf_op jit(solution)/shard_map/while/body/eval_jaxpr/ppermute | solution.py:16
  27.5 2.9 fusion.37
  30.4 5.3 %collective-permute-start = (bf16[2,384,1,128]{3,1,2,0:T(8,128)(2,1)S(1)}, bf16[2,384,1,128]{3,1,2,0:T(8,128)(2,1)S(1)}, u32[]{:S(2)}, u32[]{:S(2)}) collective-permute-start(bf16[2,384,1,128]{3,1,2,0:T(8,128)(2,1)S(1)} %get-tuple-element.306), channel_id=1, source_target_pairs={{0,8},{8,16},{16,24},{24,32},{32,40},{40,48},{48,56},{56,64},{64,7... | collective-permute-start | bytes 589832 | tf_op jit(solution)/shard_map/while/body/eval_jaxpr/ppermute | solution.py:16
  41.9 2.9 fusion.37
  44.8 5.3 %collective-permute-start = (bf16[2,384,1,128]{3,1,2,0:T(8,128)(2,1)S(1)}, bf16[2,384,1,128]{3,1,2,0:T(8,128)(2,1)S(1)}, u32[]{:S(2)}, u32[]{:S(2)}) collective-permute-start(bf16[2,384,1,128]{3,1,2,0:T(8,128)(2,1)S(1)} %get-tuple-element.306), channel_id=1, source_target_pairs={{0,8},{8,16},{16,24},{24,32},{32,40},{40,48},{48,56},{56,64},{64,7... | collective-permute-start | bytes 589832 | tf_op jit(solution)/shard_map/while/body/eval_jaxpr/ppermute | solution.py:16
  50.8 4.4 %collective-permute-done = bf16[2,384,1,128]{3,1,2,0:T(8,128)(2,1)S(1)} collective-permute-done((bf16[2,384,1,128]{3,1,2,0:T(8,128)(2,1)S(1)}, bf16[2,384,1,128]{3,1,2,0:T(8,128)(2,1)S(1)}, u32[]{:S(2)}, u32[]{:S(2)}) %collective-permute-start) | collective-permute-done | bytes 196640 | tf_op jit(solution)/shard_map/while/body/eval_jaxpr/ppermute | solution.py:16
  58.8 2.9 fusion.37
  61.7 5.3 %collective-permute-start = (bf16[2,384,1,128]{3,1,2,0:T(8,128)(2,1)S(1)}, bf16[2,384,1,128]{3,1,2,0:T(8,128)(2,1)S(1)}, u32[]{:S(2)}, u32[]{:S(2)}) collective-permute-start(bf16[2,384,1,128]{3,1,2,0:T(8,128)(2,1)S(1)} %get-tuple-element.306), channel_id=1, source_target_pairs={{0,8},{8,16},{16,24},{24,32},{32,40},{40,48},{48,56},{56,64},{64,7... | collective-permute-start | bytes 589832 | tf_op jit(solution)/shard_map/while/body/eval_jaxpr/ppermute | solution.py:16
  67.7 3.0 collective-permute-done
  74.4 2.9 fusion.37
  77.3 5.3 %collective-permute-start = (bf16[2,384,1,128]{3,1,2,0:T(8,128)(2,1)S(1)}, bf16[2,384,1,128]{3,1,2,0:T(8,128)(2,1)S(1)}, u32[]{:S(2)}, u32[]{:S(2)}) collective-permute-start(bf16[2,384,1,128]{3,1,2,0:T(8,128)(2,1)S(1)} %get-tuple-element.306), channel_id=1, source_target_pairs={{0,8},{8,16},{16,24},{24,32},{32,40},{40,48},{48,56},{56,64},{64,7... | collective-permute-start | bytes 589832 | tf_op jit(solution)/shard_map/while/body/eval_jaxpr/ppermute | solution.py:16
  83.4 5.9 %collective-permute-done = bf16[2,384,1,128]{3,1,2,0:T(8,128)(2,1)S(1)} collective-permute-done((bf16[2,384,1,128]{3,1,2,0:T(8,128)(2,1)S(1)}, bf16[2,384,1,128]{3,1,2,0:T(8,128)(2,1)S(1)}, u32[]{:S(2)}, u32[]{:S(2)}) %collective-permute-start) | collective-permute-done | bytes 196640 | tf_op jit(solution)/shard_map/while/body/eval_jaxpr/ppermute | solution.py:16
  93.0 2.9 fusion.37
  95.9 5.3 %collective-permute-start = (bf16[2,384,1,128]{3,1,2,0:T(8,128)(2,1)S(1)}, bf16[2,384,1,128]{3,1,2,0:T(8,128)(2,1)S(1)}, u32[]{:S(2)}, u32[]{:S(2)}) collective-permute-start(bf16[2,384,1,128]{3,1,2,0:T(8,128)(2,1)S(1)} %get-tuple-element.306), channel_id=1, source_target_pairs={{0,8},{8,16},{16,24},{24,32},{32,40},{40,48},{48,56},{56,64},{64,7... | collective-permute-start | bytes 589832 | tf_op jit(solution)/shard_map/while/body/eval_jaxpr/ppermute | solution.py:16
  101.9 4.1 %collective-permute-done = bf16[2,384,1,128]{3,1,2,0:T(8,128)(2,1)S(1)} collective-permute-done((bf16[2,384,1,128]{3,1,2,0:T(8,128)(2,1)S(1)}, bf16[2,384,1,128]{3,1,2,0:T(8,128)(2,1)S(1)}, u32[]{:S(2)}, u32[]{:S(2)}) %collective-permute-start) | collective-permute-done | bytes 196640 | tf_op jit(solution)/shard_map/while/body/eval_jaxpr/ppermute | solution.py:16
  109.6 2.9 fusion.37
  112.5 5.3 %collective-permute-start = (bf16[2,384,1,128]{3,1,2,0:T(8,128)(2,1)S(1)}, bf16[2,384,1,128]{3,1,2,0:T(8,128)(2,1)S(1)}, u32[]{:S(2)}, u32[]{:S(2)}) collective-permute-start(bf16[2,384,1,128]{3,1,2,0:T(8,128)(2,1)S(1)} %get-tuple-element.306), channel_id=1, source_target_pairs={{0,8},{8,16},{16,24},{24,32},{32,40},{40,48},{48,56},{56,64},{64,7... | collective-permute-start | bytes 589832 | tf_op jit(solution)/shard_map/while/body/eval_jaxpr/ppermute | solution.py:16
  118.5 3.0 collective-permute-done
  125.2 2.9 fusion.37
  128.1 5.3 %collective-permute-start = (bf16[2,384,1,128]{3,1,2,0:T(8,128)(2,1)S(1)}, bf16[2,384,1,128]{3,1,2,0:T(8,128)(2,1)S(1)}, u32[]{:S(2)}, u32[]{:S(2)}) collective-permute-start(bf16[2,384,1,128]{3,1,2,0:T(8,128)(2,1)S(1)} %get-tuple-element.306), channel_id=1, source_target_pairs={{0,8},{8,16},{16,24},{24,32},{32,40},{40,48},{48,56},{56,64},{64,7... | collective-permute-start | bytes 589832 | tf_op jit(solution)/shard_map/while/body/eval_jaxpr/ppermute | solution.py:16
  139.7 2.9 fusion.37
  142.6 5.4 %collective-permute-start = (bf16[2,384,1,128]{3,1,2,0:T(8,128)(2,1)S(1)}, bf16[2,384,1,128]{3,1,2,0:T(8,128)(2,1)S(1)}, u32[]{:S(2)}, u32[]{:S(2)}) collective-permute-start(bf16[2,384,1,128]{3,1,2,0:T(8,128)(2,1)S(1)} %get-tuple-element.306), channel_id=1, source_target_pairs={{0,8},{8,16},{16,24},{24,32},{32,40},{40,48},{48,56},{56,64},{64,7... | collective-permute-start | bytes 589832 | tf_op jit(solution)/shard_map/while/body/eval_jaxpr/ppermute | solution.py:16
  154.3 2.9 fusion.37
  157.2 5.3 %collective-permute-start = (bf16[2,384,1,128]{3,1,2,0:T(8,128)(2,1)S(1)}, bf16[2,384,1,128]{3,1,2,0:T(8,128)(2,1)S(1)}, u32[]{:S(2)}, u32[]{:S(2)}) collective-permute-start(bf16[2,384,1,128]{3,1,2,0:T(8,128)(2,1)S(1)} %get-tuple-element.306), channel_id=1, source_target_pairs={{0,8},{8,16},{16,24},{24,32},{32,40},{40,48},{48,56},{56,64},{64,7... | collective-permute-start | bytes 589832 | tf_op jit(solution)/shard_map/while/body/eval_jaxpr/ppermute | solution.py:16
  168.7 2.9 fusion.37
  171.6 5.3 %collective-permute-start = (bf16[2,384,1,128]{3,1,2,0:T(8,128)(2,1)S(1)}, bf16[2,384,1,128]{3,1,2,0:T(8,128)(2,1)S(1)}, u32[]{:S(2)}, u32[]{:S(2)}) collective-permute-start(bf16[2,384,1,128]{3,1,2,0:T(8,128)(2,1)S(1)} %get-tuple-element.306), channel_id=1, source_target_pairs={{0,8},{8,16},{16,24},{24,32},{32,40},{40,48},{48,56},{56,64},{64,7... | collective-permute-start | bytes 589832 | tf_op jit(solution)/shard_map/while/body/eval_jaxpr/ppermute | solution.py:16
  183.2 2.9 fusion.37
  186.9 14.8 %convolution_convert_fusion = bf16[384,8192]{1,0:T(8,128)(2,1)} fusion(bf16[384,1024]{0,1:T(8,128)(2,1)S(1)} %bitcast.69, bf16[1024,8192]{1,0:T(8,128)(2,1)} %all-gather.2.cloned.1.call-done), kind=kOutput, calls=%fused_computation.26 | convolution fusion | flops 6445596672 | bytes 23855104 | tf_op jit(solution)/shard_map/dot_general | solution.py:87
  201.7 124.6 %reduce-scatter.2.cloned.1.call-done = bf16[384,1024]{1,0:T(8,128)(2,1)} async-done(((bf16[384,8192]{1,0:T(8,128)(2,1)}), bf16[384,1024]{1,0:T(8,128)(2,1)}) %reduce-scatter.2.cloned.1.call-update) | async-done | bytes 786448 | tf_op jit(solution)/shard_map/reduce_scatter | solution.py:92
  (123 shorter events, 64.8 us)
Async XLA Ops:
  6.5 180.4 %all-gather.2.cloned.1.call-start = ((), (), s32[]{:S(2)}) async-start(), calls=%async_computation.1 | async-start | bytes 17301504 | tf_op jit(solution)/shard_map/all_gather | solution.py:89
  7.3 319.1 %reduce-scatter.2.cloned.1.call-start = ((), (), s32[]{:S(2)}) async-start(), calls=%async_computation.2 | async-start | bytes 7077888 | tf_op jit(solution)/shard_map/reduce_scatter | solution.py:92
  12.9 2.0 copy-start
  17.1 6.7 %collective-permute-start = (bf16[2,384,1,128]{3,1,2,0:T(8,128)(2,1)S(1)}, bf16[2,384,1,128]{3,1,2,0:T(8,128)(2,1)S(1)}, u32[]{:S(2)}, u32[]{:S(2)}) collective-permute-start(bf16[2,384,1,128]{3,1,2,0:T(8,128)(2,1)S(1)} %get-tuple-element.306), channel_id=1, source_target_pairs={{0,8},{8,16},{16,24},{24,32},{32,40},{40,48},{48,56},{56,64},{64,7... | collective-permute-start | bytes 589832 | tf_op jit(solution)/shard_map/while/body/eval_jaxpr/ppermute | solution.py:16
  30.4 7.9 %collective-permute-start = (bf16[2,384,1,128]{3,1,2,0:T(8,128)(2,1)S(1)}, bf16[2,384,1,128]{3,1,2,0:T(8,128)(2,1)S(1)}, u32[]{:S(2)}, u32[]{:S(2)}) collective-permute-start(bf16[2,384,1,128]{3,1,2,0:T(8,128)(2,1)S(1)} %get-tuple-element.306), channel_id=1, source_target_pairs={{0,8},{8,16},{16,24},{24,32},{32,40},{40,48},{48,56},{56,64},{64,7... | collective-permute-start | bytes 589832 | tf_op jit(solution)/shard_map/while/body/eval_jaxpr/ppermute | solution.py:16
  44.8 10.4 %collective-permute-start = (bf16[2,384,1,128]{3,1,2,0:T(8,128)(2,1)S(1)}, bf16[2,384,1,128]{3,1,2,0:T(8,128)(2,1)S(1)}, u32[]{:S(2)}, u32[]{:S(2)}) collective-permute-start(bf16[2,384,1,128]{3,1,2,0:T(8,128)(2,1)S(1)} %get-tuple-element.306), channel_id=1, source_target_pairs={{0,8},{8,16},{16,24},{24,32},{32,40},{40,48},{48,56},{56,64},{64,7... | collective-permute-start | bytes 589832 | tf_op jit(solution)/shard_map/while/body/eval_jaxpr/ppermute | solution.py:16
  61.7 9.0 %collective-permute-start = (bf16[2,384,1,128]{3,1,2,0:T(8,128)(2,1)S(1)}, bf16[2,384,1,128]{3,1,2,0:T(8,128)(2,1)S(1)}, u32[]{:S(2)}, u32[]{:S(2)}) collective-permute-start(bf16[2,384,1,128]{3,1,2,0:T(8,128)(2,1)S(1)} %get-tuple-element.306), channel_id=1, source_target_pairs={{0,8},{8,16},{16,24},{24,32},{32,40},{40,48},{48,56},{56,64},{64,7... | collective-permute-start | bytes 589832 | tf_op jit(solution)/shard_map/while/body/eval_jaxpr/ppermute | solution.py:16
  77.3 12.0 %collective-permute-start = (bf16[2,384,1,128]{3,1,2,0:T(8,128)(2,1)S(1)}, bf16[2,384,1,128]{3,1,2,0:T(8,128)(2,1)S(1)}, u32[]{:S(2)}, u32[]{:S(2)}) collective-permute-start(bf16[2,384,1,128]{3,1,2,0:T(8,128)(2,1)S(1)} %get-tuple-element.306), channel_id=1, source_target_pairs={{0,8},{8,16},{16,24},{24,32},{32,40},{40,48},{48,56},{56,64},{64,7... | collective-permute-start | bytes 589832 | tf_op jit(solution)/shard_map/while/body/eval_jaxpr/ppermute | solution.py:16
  95.9 10.1 %collective-permute-start = (bf16[2,384,1,128]{3,1,2,0:T(8,128)(2,1)S(1)}, bf16[2,384,1,128]{3,1,2,0:T(8,128)(2,1)S(1)}, u32[]{:S(2)}, u32[]{:S(2)}) collective-permute-start(bf16[2,384,1,128]{3,1,2,0:T(8,128)(2,1)S(1)} %get-tuple-element.306), channel_id=1, source_target_pairs={{0,8},{8,16},{16,24},{24,32},{32,40},{40,48},{48,56},{56,64},{64,7... | collective-permute-start | bytes 589832 | tf_op jit(solution)/shard_map/while/body/eval_jaxpr/ppermute | solution.py:16
  112.5 9.0 %collective-permute-start = (bf16[2,384,1,128]{3,1,2,0:T(8,128)(2,1)S(1)}, bf16[2,384,1,128]{3,1,2,0:T(8,128)(2,1)S(1)}, u32[]{:S(2)}, u32[]{:S(2)}) collective-permute-start(bf16[2,384,1,128]{3,1,2,0:T(8,128)(2,1)S(1)} %get-tuple-element.306), channel_id=1, source_target_pairs={{0,8},{8,16},{16,24},{24,32},{32,40},{40,48},{48,56},{56,64},{64,7... | collective-permute-start | bytes 589832 | tf_op jit(solution)/shard_map/while/body/eval_jaxpr/ppermute | solution.py:16
  128.1 7.9 %collective-permute-start = (bf16[2,384,1,128]{3,1,2,0:T(8,128)(2,1)S(1)}, bf16[2,384,1,128]{3,1,2,0:T(8,128)(2,1)S(1)}, u32[]{:S(2)}, u32[]{:S(2)}) collective-permute-start(bf16[2,384,1,128]{3,1,2,0:T(8,128)(2,1)S(1)} %get-tuple-element.306), channel_id=1, source_target_pairs={{0,8},{8,16},{16,24},{24,32},{32,40},{40,48},{48,56},{56,64},{64,7... | collective-permute-start | bytes 589832 | tf_op jit(solution)/shard_map/while/body/eval_jaxpr/ppermute | solution.py:16
  142.6 8.0 %collective-permute-start = (bf16[2,384,1,128]{3,1,2,0:T(8,128)(2,1)S(1)}, bf16[2,384,1,128]{3,1,2,0:T(8,128)(2,1)S(1)}, u32[]{:S(2)}, u32[]{:S(2)}) collective-permute-start(bf16[2,384,1,128]{3,1,2,0:T(8,128)(2,1)S(1)} %get-tuple-element.306), channel_id=1, source_target_pairs={{0,8},{8,16},{16,24},{24,32},{32,40},{40,48},{48,56},{56,64},{64,7... | collective-permute-start | bytes 589832 | tf_op jit(solution)/shard_map/while/body/eval_jaxpr/ppermute | solution.py:16
  157.2 7.9 %collective-permute-start = (bf16[2,384,1,128]{3,1,2,0:T(8,128)(2,1)S(1)}, bf16[2,384,1,128]{3,1,2,0:T(8,128)(2,1)S(1)}, u32[]{:S(2)}, u32[]{:S(2)}) collective-permute-start(bf16[2,384,1,128]{3,1,2,0:T(8,128)(2,1)S(1)} %get-tuple-element.306), channel_id=1, source_target_pairs={{0,8},{8,16},{16,24},{24,32},{32,40},{40,48},{48,56},{56,64},{64,7... | collective-permute-start | bytes 589832 | tf_op jit(solution)/shard_map/while/body/eval_jaxpr/ppermute | solution.py:16
  171.6 7.9 %collective-permute-start = (bf16[2,384,1,128]{3,1,2,0:T(8,128)(2,1)S(1)}, bf16[2,384,1,128]{3,1,2,0:T(8,128)(2,1)S(1)}, u32[]{:S(2)}, u32[]{:S(2)}) collective-permute-start(bf16[2,384,1,128]{3,1,2,0:T(8,128)(2,1)S(1)} %get-tuple-element.306), channel_id=1, source_target_pairs={{0,8},{8,16},{16,24},{24,32},{32,40},{40,48},{48,56},{56,64},{64,7... | collective-permute-start | bytes 589832 | tf_op jit(solution)/shard_map/while/body/eval_jaxpr/ppermute | solution.py:16
Sparse Core Ops, SparseCore 0:
  9.1 134.1 all-gather.1
  201.8 124.4 reduce-scatter.1
where the time goes:
time: 336 us; the launch traced here: 333 us
  waiting for transfers between devices  157 us (47%)
  matrix products  69 us (21%)
  starting transfers between devices  57.2 us (17%)
  other arithmetic  32.6 us (10%)
  between operations  14.2 us (4%)
    reduce_scatter x1, waiting for transfers between devices, body(): lax.psum_scatter(partial_sums.astype(jnp.bfloat16), 'head', scatter_dimen...  125 us
    ppermute x11, starting transfers between devices, passed_along(): return lax.ppermute(block, axis, route)  57.2 us
    dot_general x12, matrix products, attend(): jnp.einsum('qki,iqx->qkx', weights.astype(jnp.bfloat16), query_key_block_...  33.7 us
    ppermute x11, waiting for transfers between devices, passed_along(): return lax.ppermute(block, axis, route)  31.8 us
    reduce_sum x12, other arithmetic, attend(): total = total * rescale + jnp.sum(weights, axis=2)  23.1 us
    dot_general x12, matrix products, attend(): jnp.einsum('yzf,wyf->yzw', query_row_matrix, query_key_block_couple[0], p...  20.6 us
    dot_general x1, matrix products, body(): jnp.dot(attended, lax.all_gather(out_weight, 'seq', axis=1, tiled=True),...  14.8 us
    add x12, other arithmetic, body(): start_pos + jnp.arange(QPG * tok_rows, dtype=jnp.int32) % tok_rows  7.27 us
  transfers between devices with their start and end apart: 13, of which 12 were waited for; matrix products, arithmetic and copies ran while one was open for 27% of the time, Pallas kernels for 0%

commit v1 on v0

v1 whole, which is shorter than its diff:
```python
import math

import jax
import jax.numpy as jnp
from jax import lax
from jax.experimental import pallas as pl
from jax.experimental.pallas import tpu as pltpu
from jax.sharding import PartitionSpec as P

MESH = pl.DeviceIdType.MESH
DH = 128
QPG = 8
T = 384
NZ = 8
NEG = -1e30
ROWS = 2 * T
PAIRS = QPG // 2
VR = DH + 16
C = 256
F32 = jnp.float32
BF16 = jnp.bfloat16
NT = (((1,), (1,)), ((), ()))
NN = (((1,), (0,)), ((), ()))


def dot(a, b, dims=NN):
    return lax.dot_general(a, b, dims, preferred_element_type=F32)


def kernel(q_ref, k_ref, v_ref, win_ref, w_ref, out_ref,
           qs, k_all, vt_all, w_all, a_all, s_ref, m_ref, acc_ref, fb_ref, bias0, kb, vb, tb,
           tx, rx, keep, xtx, xrx, fin,
           lsem, zs, zr, xs, xr, ss, sr, fs, fr, wds, wdr, wus, wur,
           axs, axr, ass, asr, afs, afr, ys, yr, hs, hr, os, orr):
    seq = lax.axis_index("seq")
    head = lax.axis_index("head")
    z = seq // 4
    q = seq % 4
    y = head // 2
    xh = head % 2
    q1 = q + 1 - 2 * (q % 2)
    q2 = (q + 2) % 4
    q3 = q1 + 2 - 4 * (q1 // 2)
    zup = (((z + 1) % NZ) * 4 + q, head)
    zdn = (((z + NZ - 1) % NZ) * 4 + q, head)
    sib = (z * 4 + q1, head)
    xlo = (z * 4 + q2, head)
    dia = (z * 4 + q3, head)
    yup = (seq, ((y + 1) % 4) * 2 + xh)
    ydn = (seq, ((y + 3) % 4) * 2 + xh)
    xhi = (seq, y * 2 + 1 - xh)

    def rc(src, dst, ssem, rsem, dev):
        return pltpu.make_async_remote_copy(
            src_ref=src, dst_ref=dst, send_sem=ssem, recv_sem=rsem, device_id=dev, device_id_type=MESH)

    lk = pltpu.make_async_copy(k_ref, k_all.at[3], lsem.at[0])
    lw = pltpu.make_async_copy(w_ref, w_all.at[0], lsem.at[1])
    lk.start()
    lw.start()
    barrier = pltpu.get_barrier_semaphore()
    for dev in (zup, zdn, sib, xlo, dia, yup, ydn, xhi):
        pl.semaphore_signal(barrier, inc=1, device_id=dev, device_id_type=MESH)
    for slot in range(19):
        vt_all[slot, DH:VR, :] = jnp.ones((VR - DH, T), BF16)
    vt_all[3, 0:DH, :] = v_ref[...].astype(F32).T.astype(BF16)
    lk.wait()
    lw.wait()
    pl.semaphore_wait(barrier, 8)

    def kv(src_slot, dst_slot, ssem, rsem, n, dev):
        return (rc(k_all.at[src_slot], k_all.at[dst_slot], ssem.at[n, 0], rsem.at[n, 0], dev),
                rc(vt_all.at[src_slot, pl.ds(0, DH)], vt_all.at[dst_slot, pl.ds(0, DH)],
                   ssem.at[n, 1], rsem.at[n, 1], dev))

    def kv_z(dz):
        return kv(3 + 4 * dz, 7 + 4 * dz, zs, zr, dz, zup)

    def kv_x(dz):
        return kv(3 + 4 * dz, 3 + 4 * dz + q2 - q, xs, xr, dz, xlo)

    def kv_s(dz):
        return kv(3 + 4 * dz, 3 + 4 * dz + q1 - q, ss, sr, dz, sib)

    def kv_f(dz):
        return kv(3 + 4 * dz + q - q2, 3 + 4 * dz + q1 - q2, fs, fr, dz, sib)

    def w_dn(n):
        return rc(w_all.at[n], w_all.at[n + 1], wds.at[n], wdr.at[n], zdn)

    def w_up(n):
        return rc(w_all.at[(NZ - n) % NZ], w_all.at[NZ - 1 - n], wus.at[n], wur.at[n], zup)

    def start(*copies):
        for c in copies:
            c.start()

    def got(*copies):
        for c in copies:
            c.wait_recv()

    start(*kv_z(0), *kv_x(0), *kv_s(0))
    start(w_dn(0))

    for p in range(QPG):
        qs[p // 2, (p % 2) * T:(p % 2 + 1) * T, :] = (
            q_ref[:, p * DH:(p + 1) * DH].astype(F32) * (math.log2(math.e) / math.sqrt(DH))).astype(BF16)
    wn = win_ref[0] // 128
    col = lax.broadcasted_iota(jnp.int32, (1, ROWS), 1)
    ctile = sum(jnp.where(col >= 128 * n, 1, 0) for n in range(1, 6))
    iq = ctile - 3 * jnp.where(ctile >= 3, 1, 0)
    for d in range(1, 12):
        for jk in range(3):
            inside = (3 * d - jk + iq < wn) & (seq - d >= 0)
            fb_ref[d * 3 + jk] = jnp.where(inside, 0.0, NEG)
    kj = lax.broadcasted_iota(jnp.int32, (T, T), 0)
    qi = lax.broadcasted_iota(jnp.int32, (T, T), 1)
    kt = jnp.where(kj >= 128, 1, 0) + jnp.where(kj >= 256, 1, 0)
    qt = jnp.where(qi >= 128, 1, 0) + jnp.where(qi >= 256, 1, 0)
    bias0[...] = jnp.where((kj <= qi) & (qt - kt < wn), 0.0, NEG)

    def group(dlist, first, last):
        def pair_body(pr, carry):
            qp = qs[pr]
            mx = None
            for b, d in enumerate(dlist):
                s = dot(k_all[d + 3], qp, NT)
                if d == 0:
                    s = s + jnp.concatenate([bias0[...], bias0[...]], axis=1)
                s_ref[b] = s
                for jk in range(3):
                    t8 = jnp.max(s[jk * 128:(jk + 1) * 128].reshape(16, 8, ROWS), axis=0)
                    if d > 0:
                        t8 = t8 + fb_ref[d * 3 + jk]
                    mx = t8 if mx is None else jnp.maximum(mx, t8)
            edge = []
            if last:
                for c in range(6):
                    sb = dot(kb[c % 3], qp[c * 128:(c + 1) * 128], NT) + tb[c % 3]
                    edge.append(sb)
                e8 = [jnp.max(sb.reshape(16, 8, 128), axis=0) for sb in edge]
                mx = jnp.maximum(mx, jnp.concatenate(e8, axis=1))
            m_new = jnp.max(mx, axis=0, keepdims=True)
            if not first:
                m_old = m_ref[pr]
                m_new = jnp.maximum(m_old, m_new)
                alpha = jnp.exp2(m_old - m_new)
            pv = None
            for b, d in enumerate(dlist):
                tiles = []
                for jk in range(3):
                    shift = m_new - fb_ref[d * 3 + jk] if d > 0 else m_new
                    tiles.append(jnp.exp2(s_ref[b, jk * 128:(jk + 1) * 128, :] - shift).astype(BF16))
                part = dot(vt_all[d + 3], jnp.concatenate(tiles, axis=0))
                pv = part if pv is None else pv + part
            if last:
                ep = []
                for c in range(6):
                    pe = jnp.exp2(edge[c] - m_new[:, c * 128:(c + 1) * 128]).astype(BF16)
                    ep.append(dot(vb[c % 3], pe))
                pv = pv + jnp.concatenate(ep, axis=1)
            if not first:
                pv = acc_ref[pr] * alpha + pv
            if last:
                o = pv[0:DH] / pv[DH:DH + 1]
                for h in range(2):
                    a_all[q, pr, :, h * DH:(h + 1) * DH] = o[:, h * T:(h + 1) * T].T.astype(BF16)
                start(a_x(pr), a_s(pr))
            else:
                acc_ref[pr] = pv
                m_ref[pr] = m_new
            return carry

        lax.fori_loop(0, PAIRS, pair_body, 0)

    def a_x(pr):
        return rc(a_all.at[q, pr], a_all.at[q, pr], axs.at[pr], axr.at[pr], xlo)

    def a_s(pr):
        return rc(a_all.at[q, pr], a_all.at[q, pr], ass.at[pr], asr.at[pr], sib)

    def a_f(pr):
        return rc(a_all.at[q2, pr], a_all.at[q2, pr], afs.at[pr], afr.at[pr], sib)

    group((0,), True, False)
    got(*kv_z(0))
    start(*kv_z(1), *kv_x(1), *kv_s(1))
    got(*kv_x(0))
    start(*kv_f(0))
    got(*kv_z(1))
    start(*kv_z(2), *kv_x(2), *kv_s(2))
    start(w_up(0))
    got(*kv_x(1))
    start(*kv_f(1))
    got(*kv_s(0), *kv_s(1), *kv_f(0), *kv_f(1))
    group((1, 2, 3), False, False)
    got(w_dn(0))
    start(w_dn(1))
    got(*kv_z(2))
    start(*kv_x(3), *kv_s(3))
    got(*kv_x(2))
    start(*kv_f(2))
    got(*kv_s(2), *kv_f(2))
    group((4, 5, 6, 7), False, False)
    got(*kv_x(3))
    start(*kv_f(3))
    got(*kv_s(3), *kv_f(3))
    got(w_dn(1))
    start(w_dn(2))
    got(w_up(0))
    start(w_up(1))
    ej = lax.broadcasted_iota(jnp.int32, (128, 128), 0)
    ei = lax.broadcasted_iota(jnp.int32, (128, 128), 1)
    for n in range(3):
        kn = jnp.zeros((128, DH), BF16)
        vn = jnp.zeros((VR, 128), BF16)
        for d in range(12):
            for jk in range(3):
                if 2 <= 3 * d + n - jk <= 32:
                    here = wn == 3 * d + n - jk
                    kn = jnp.where(here, k_all[d + 3, jk * 128:(jk + 1) * 128, :], kn)
                    vn = jnp.where(here, vt_all[d + 3, :, jk * 128:(jk + 1) * 128], vn)
        kb[n] = kn
        vb[n] = vn
        tb[n] = jnp.where((ej > ei) & (3 * seq + n - wn >= 0), 0.0, NEG)
    group((8, 9, 10, 11), False, True)

    for pr in range(PAIRS):
        got(a_x(pr))
        start(a_f(pr))
    got(w_dn(2))
    start(w_dn(3))
    got(w_up(1))
    start(w_up(2))
    for pr in range(PAIRS):
        got(a_s(pr), a_f(pr))
    got(w_dn(3), w_up(2))

    def ycopy(rb, way, n):
        return rc(tx.at[rb, way, n], rx.at[rb, way, n], ys.at[rb, way, n], yr.at[rb, way, n], yup if way == 0 else ydn)

    def hcopy(rb):
        return rc(xtx.at[rb], xrx.at[rb], hs.at[rb], hr.at[rb], xhi)

    def ocopy(rb, dev_q, slot):
        cols = pl.ds(pl.multiple_of(slot * C, C), C)
        return rc(fin.at[rb], out_ref.at[:, cols], os.at[rb], orr.at[slot], (z * 4 + dev_q, head))

    def project(rb, yd, half):
        r = (((y + yd) % 4) * 2 + half + NZ - z) % NZ
        total = None
        for pr in range(PAIRS):
            part = dot(a_all[rb, pr], w_all[r, pr * C:(pr + 1) * C, :])
            total = part if total is None else total + part
        return total

    def first_stage(rb):
        for way in range(2):
            tx[rb, way, 0] = project(rb, 2, way).astype(BF16)
            start(ycopy(rb, way, 0))
        for way in range(2):
            tx[rb, way, 1] = project(rb, 1 if way == 0 else 3, 1 - way).astype(BF16)
            start(ycopy(rb, way, 1))
        for way in range(2):
            keep[rb, way] = project(rb, 1 if way == 0 else 3, way)
        for half in range(2):
            keep[rb, 2 + half] = project(rb, 0, half)

    def second_stage(rb):
        for way in range(2):
            got(ycopy(rb, way, 0))
            tx[rb, way, 2] = (keep[rb, way] + rx[rb, way, 0].astype(F32)).astype(BF16)
            start(ycopy(rb, way, 2))

    def third_stage(rb):
        for n in (1, 2):
            for way in range(2):
                got(ycopy(rb, way, n))
        for half in range(2):
            keep[rb, 2 + half] = keep[rb, 2 + half] + (
                rx[rb, half, 2].astype(F32) + rx[rb, 1 - half, 1].astype(F32))
        xtx[rb] = keep[rb, 3 - xh].astype(BF16)
        start(hcopy(rb))

    def fourth_stage(rb):
        got(hcopy(rb))
        total = (keep[rb, 2 + xh] + xrx[rb].astype(F32)).astype(BF16)
        fin[rb] = total

        @pl.when(rb != q)
        def _():
            start(ocopy(rb, rb, q))

    def rb_loop(t, carry):
        for lag, (stage) in enumerate((first_stage, second_stage, third_stage, fourth_stage)):
            @pl.when((t >= lag) & (t < 4 + lag))
            def _():
                stage(t - lag)
        return carry

    lax.fori_loop(0, 7, rb_loop, 0)
    out_ref[:, pl.ds(pl.multiple_of(q * C, C), C)] = fin[q]

    for c in kv_z(0) + kv_z(1) + kv_z(2):
        c.wait_send()
    for dz in range(4):
        for c in kv_x(dz) + kv_s(dz) + kv_f(dz):
            c.wait_send()
    for n in range(4):
        w_dn(n).wait_send()
    for n in range(3):
        w_up(n).wait_send()
    for pr in range(PAIRS):
        for c in (a_x(pr), a_s(pr), a_f(pr)):
            c.wait_send()

    def finish(rb, carry):
        for way in range(2):
            for n in range(3):
                ycopy(rb, way, n).wait_send()
        hcopy(rb).wait_send()

        @pl.when(rb != q)
        def _():
            ocopy(rb, rb, q).wait_send()
            ocopy(rb, rb, rb).wait_recv()

        return carry

    lax.fori_loop(0, 4, finish, 0)


def body(queries, keys, values, windows, out_weight):
    dma = pltpu.SemaphoreType.DMA
    vm = pl.BlockSpec(memory_space=pltpu.VMEM)
    hbm = pl.BlockSpec(memory_space=pl.ANY)
    return pl.pallas_call(
        kernel,
        out_shape=jax.ShapeDtypeStruct((T, 4 * C), BF16),
        in_specs=[vm, hbm, vm, pl.BlockSpec(memory_space=pltpu.SMEM), hbm],
        out_specs=vm,
        scratch_shapes=[
            pltpu.VMEM((PAIRS, ROWS, DH), BF16),
            pltpu.VMEM((19, T, DH), BF16),
            pltpu.VMEM((19, VR, T), BF16),
            pltpu.VMEM((NZ, QPG * DH, C), BF16),
            pltpu.VMEM((4, PAIRS, T, C), BF16),
            pltpu.VMEM((4, T, ROWS), F32),
            pltpu.VMEM((PAIRS, 1, ROWS), F32),
            pltpu.VMEM((PAIRS, VR, ROWS), F32),
            pltpu.VMEM((36, 1, ROWS), F32),
            pltpu.VMEM((T, T), F32),
            pltpu.VMEM((3, 128, DH), BF16),
            pltpu.VMEM((3, VR, 128), BF16),
            pltpu.VMEM((3, 128, 128), F32),
            pltpu.VMEM((4, 2, 3, T, C), BF16),
            pltpu.VMEM((4, 2, 3, T, C), BF16),
            pltpu.VMEM((4, 4, T, C), F32),
            pltpu.VMEM((4, T, C), BF16),
            pltpu.VMEM((4, T, C), BF16),
            pltpu.VMEM((4, T, C), BF16),
            dma((2,)),
            dma((3, 2)), dma((3, 2)),
            dma((4, 2)), dma((4, 2)),
            dma((4, 2)), dma((4, 2)),
            dma((4, 2)), dma((4, 2)),
            dma((4,)), dma((4,)),
            dma((3,)), dma((3,)),
            dma((PAIRS,)), dma((PAIRS,)),
            dma((PAIRS,)), dma((PAIRS,)),
            dma((PAIRS,)), dma((PAIRS,)),
            dma((4, 2, 3)), dma((4, 2, 3)),
            dma((4,)), dma((4,)),
            dma((4,)), dma((4,)),
        ],
        compiler_params=pltpu.CompilerParams(
            collective_id=0, has_side_effects=True, vmem_limit_bytes=60 * 1024 * 1024),
        name="fused",
    )(queries, keys, values, windows, out_weight)


def solution(mesh):
    placed = (P("seq", "head"), P("seq", "head"), P("seq", "head"), P("head"), P("head", "seq"))
    return jax.shard_map(
        body, mesh=mesh, in_specs=placed, out_specs=P("seq", "head"), check_vma=False
    )
```

time: 336 us -> 149 us (0.44)
  waiting for transfers between devices: 157 us -> 0 us
  Pallas kernels: 0 us -> 146 us
  matrix products: 69 us -> 0 us
  starting transfers between devices: 57.2 us -> 0 us
  other arithmetic: 32.6 us -> 0 us
  between operations: 14.2 us -> 0.66 us
    pallas_call x0 -> x1, Pallas kernels: none -> 146 us  [body(): pl.pallas_call(kernel, out_shape=jax.ShapeDtypeStruct((T, 4 * C), BF16),...]
    reduce_scatter x1 -> x0, waiting for transfers between devices: 125 us -> none  [body(): lax.psum_scatter(partial_sums.astype(jnp.bfloat16), 'head', scatter_dimen...]
    dot_general x25 -> x0, matrix products: 69 us -> none  [the longest x12 33.7 us: attend(): jnp.einsum('qki,iqx->qkx', weights.astype(jnp.bfloat16), query_key_block_...]
    ppermute x11 -> x0, starting transfers between devices: 57.2 us -> none  [passed_along(): return lax.ppermute(block, axis, route)]
    ppermute x11 -> x0, waiting for transfers between devices: 31.8 us -> none  [passed_along(): return lax.ppermute(block, axis, route)]
    reduce_sum x12 -> x0, other arithmetic: 23.1 us -> none  [attend(): total = total * rescale + jnp.sum(weights, axis=2)]
    add x36 -> x0, other arithmetic: 7.83 us -> none  [the longest x12 7.27 us: body(): start_pos + jnp.arange(QPG * tok_rows, dtype=jnp.int32) % tok_rows]
  transfers between devices with their start and end apart: 13 -> 0, of which waited for: 12 -> 0; matrix products, arithmetic and copies ran while one was open for 27% -> 0% of each run, Pallas kernels for 0% -> 0%
where the time goes in v1:
time: 149 us
  Pallas kernels  146 us (98%)
  local copies, waits for them, and re-layouts  2.06 us (1%)
    pallas_call x1, Pallas kernels, body(): pl.pallas_call(kernel, out_shape=jax.ShapeDtypeStruct((T, 4 * C), BF16),...  146 us

profile of v1, /device:TPU:3, one launch (start us, length us, event | category | flops | bytes accessed | tf_op | source)
XLA Modules:
  0.0 148.9 jit_solution(11906976917658933869)
XLA Ops:
  0.7 146.2 %fused.1 = bf16[384,1024]{1,0:T(8,128)(2,1)} custom-call(bf16[384,1024]{1,0:T(8,128)(2,1)} %q_ref.1, bf16[384,128]{1,0:T(8,128)(2,1)} %k_ref.1, bf16[384,128]{1,0:T(8,128)(2,1)} %v_ref.1, s32[1]{0:T(128)S(6)} %copy.7.win_ref, bf16[1024,256]{1,0:T(8,128)(2,1)} %w_ref.1), custom_call_target="tpu_custom_call" | custom-call | tf_op jit(solution)/shard_map/fused/pallas_call | solution.py:337
  146.9 2.1 %copy.8 = bf16[384,1024]{1,0:T(8,128)(2,1)} copy(bf16[384,1024]{1,0:T(8,128)(2,1)} %fused.1) | data formatting | bytes 1572864

commit v2 on v1

--- a/solution.py
+++ b/solution.py
@@ -12,6 +12,7 @@
 QPG = 8
 T = 384
 NZ = 8
+H = T // 2
 NEG = -1e30
 ROWS = 2 * T
 PAIRS = QPG // 2
@@ -68,28 +69,58 @@
     lw.wait()
     pl.semaphore_wait(barrier, 8)
 
-    def kv(src_slot, dst_slot, ssem, rsem, n, dev):
-        return (rc(k_all.at[src_slot], k_all.at[dst_slot], ssem.at[n, 0], rsem.at[n, 0], dev),
-                rc(vt_all.at[src_slot, pl.ds(0, DH)], vt_all.at[dst_slot, pl.ds(0, DH)],
-                   ssem.at[n, 1], rsem.at[n, 1], dev))
-
-    def kv_z(dz):
-        return kv(3 + 4 * dz, 7 + 4 * dz, zs, zr, dz, zup)
-
-    def kv_x(dz):
-        return kv(3 + 4 * dz, 3 + 4 * dz + q2 - q, xs, xr, dz, xlo)
-
-    def kv_s(dz):
-        return kv(3 + 4 * dz, 3 + 4 * dz + q1 - q, ss, sr, dz, sib)
-
-    def kv_f(dz):
-        return kv(3 + 4 * dz + q - q2, 3 + 4 * dz + q1 - q2, fs, fr, dz, sib)
-
-    def w_dn(n):
-        return rc(w_all.at[n], w_all.at[n + 1], wds.at[n], wdr.at[n], zdn)
-
-    def w_up(n):
-        return rc(w_all.at[(NZ - n) % NZ], w_all.at[NZ - 1 - n], wus.at[n], wur.at[n], zup)
+    def kv(src_slot, dst_slot, ssem, rsem, n, i, dev):
+        if i == 0:
+            return rc(k_all.at[src_slot], k_all.at[dst_slot], ssem.at[n, 0], rsem.at[n, 0], dev)
+        return rc(vt_all.at[src_slot, pl.ds(0, DH)], vt_all.at[dst_slot, pl.ds(0, DH)],
+                  ssem.at[n, 1], rsem.at[n, 1], dev)
+
+    def kv_z(dz, i):
+        return kv(3 + 4 * dz, 7 + 4 * dz, zs, zr, dz, i, zup)
+
+    def kv_x(dz, i):
+        return kv(3 + 4 * dz, 3 + 4 * dz + q2 - q, xs, xr, dz, i, xlo)
+
+    def kv_s(dz, i):
+        return kv(3 + 4 * dz, 3 + 4 * dz + q1 - q, ss, sr, dz, i, sib)
+
+    def kv_f(dz, i):
+        return kv(3 + 4 * dz + q - q2, 3 + 4 * dz + q1 - q2, fs, fr, dz, i, sib)
+
+    def only(dz, near, far, act):
+        if dz in (1, 2):
+            act()
+        else:
+            pl.when(near if dz == 0 else far)(act)
+
+    low, even = q < 2, q % 2 == 0
+    high, odd = q >= 2, q % 2 == 1
+
+    def send_z(dz, i):
+        kv_z(dz, i).start()
+
+    def send_xs(dz, i):
+        only(dz, low, high, lambda: kv_x(dz, i).start())
+        only(dz, even, odd, lambda: kv_s(dz, i).start())
+
+    def pass_f(dz, i):
+        def act():
+            kv_x(dz, i).wait_recv()
+            kv_f(dz, i).start()
+        only(dz, high, low, act)
+
+    def got_sf(dz):
+        for i in range(2):
+            only(dz, odd, even, lambda: kv_s(dz, i).wait_recv())
+            only(dz, high, low, lambda: kv_f(dz, i).wait_recv())
+
+    def w_dn(n, hf):
+        rows = pl.ds(hf * 256, 256)
+        return rc(w_all.at[n, rows], w_all.at[n + 1, rows], wds.at[n, hf], wdr.at[n, hf], zdn)
+
+    def w_up(n, hf):
+        rows = pl.ds(hf * 256, 256)
+        return rc(w_all.at[(NZ - n) % NZ, rows], w_all.at[NZ - 1 - n, rows], wus.at[n, hf], wur.at[n, hf], zup)
 
     def start(*copies):
         for c in copies:
@@ -99,8 +130,18 @@
         for c in copies:
             c.wait_recv()
 
-    start(*kv_z(0), *kv_x(0), *kv_s(0))
-    start(w_dn(0))
+    def pass_dn(n, hf):
+        got(w_dn(n, hf))
+        start(w_dn(n + 1, hf))
+
+    def pass_up(n, hf):
+        got(w_up(n, hf))
+        start(w_up(n + 1, hf))
+
+    for i in range(2):
+        send_z(0, i)
+        send_xs(0, i)
+    start(*[w_dn(0, hf) for hf in range(4)], w_up(0, 0))
 
     for p in range(QPG):
         qs[p // 2, (p % 2) * T:(p % 2 + 1) * T, :] = (
@@ -119,8 +160,10 @@
     qt = jnp.where(qi >= 128, 1, 0) + jnp.where(qi >= 256, 1, 0)
     bias0[...] = jnp.where((kj <= qi) & (qt - kt < wn), 0.0, NEG)
 
-    def group(dlist, first, last):
+    def group(dlist, first, last, service=()):
         def pair_body(pr, carry):
+            for at, act in service:
+                pl.when(pr == at)(act)
             qp = qs[pr]
             mx = None
             for b, d in enumerate(dlist):
@@ -183,32 +226,62 @@
         return rc(a_all.at[q2, pr], a_all.at[q2, pr], afs.at[pr], afr.at[pr], sib)
 
     group((0,), True, False)
-    got(*kv_z(0))
-    start(*kv_z(1), *kv_x(1), *kv_s(1))
-    got(*kv_x(0))
-    start(*kv_f(0))
-    got(*kv_z(1))
-    start(*kv_z(2), *kv_x(2), *kv_s(2))
-    start(w_up(0))
-    got(*kv_x(1))
-    start(*kv_f(1))
-    got(*kv_s(0), *kv_s(1), *kv_f(0), *kv_f(1))
-    group((1, 2, 3), False, False)
-    got(w_dn(0))
-    start(w_dn(1))
-    got(*kv_z(2))
-    start(*kv_x(3), *kv_s(3))
-    got(*kv_x(2))
-    start(*kv_f(2))
-    got(*kv_s(2), *kv_f(2))
-    group((4, 5, 6, 7), False, False)
-    got(*kv_x(3))
-    start(*kv_f(3))
-    got(*kv_s(3), *kv_f(3))
-    got(w_dn(1))
-    start(w_dn(2))
-    got(w_up(0))
-    start(w_up(1))
+    for i in range(2):
+        got(kv_z(0, i))
+        send_z(1, i)
+        send_xs(1, i)
+    start(w_up(0, 1))
+    for i in range(2):
+        pass_f(0, i)
+    for i in range(2):
+        got(kv_z(1, i))
+        send_z(2, i)
+        send_xs(2, i)
+    start(w_up(0, 2), w_up(0, 3))
+    pass_dn(0, 0)
+    pass_dn(0, 1)
+    for i in range(2):
+        pass_f(1, i)
+    pass_dn(0, 2)
+    got_sf(0)
+    got_sf(1)
+
+    def in_first():
+        for i in range(2):
+            got(kv_z(2, i))
+            send_xs(3, i)
+        pass_dn(0, 3)
+        pass_up(0, 0)
+
+    group((1, 2, 3), False, False, ((2, in_first),))
+    for i in range(2):
+        pass_f(2, i)
+    pass_dn(1, 0)
+    got_sf(2)
+
+    def in_second():
+        pass_dn(1, 1)
+        pass_up(0, 1)
+        for i in range(2):
+            pass_f(3, i)
+
+    def late_second():
+        pass_dn(1, 2)
+        pass_up(0, 2)
+
+    group((4, 5, 6, 7), False, False, ((1, in_second), (3, late_second)))
+    got_sf(3)
+    pass_dn(1, 3)
+    pass_up(0, 3)
+
+    def in_third():
+        pass_dn(2, 0)
+        pass_up(1, 0)
+
+    def late_third():
+        pass_dn(2, 1)
+        pass_up(1, 1)
+
     ej = lax.broadcasted_iota(jnp.int32, (128, 128), 0)
     ei = lax.broadcasted_iota(jnp.int32, (128, 128), 1)
     for n in range(3):
@@ -223,18 +296,17 @@
         kb[n] = kn
         vb[n] = vn
         tb[n] = jnp.where((ej > ei) & (3 * seq + n - wn >= 0), 0.0, NEG)
-    group((8, 9, 10, 11), False, True)
-
+    group((8, 9, 10, 11), False, True, ((1, in_third), (3, late_third)))
+    for hf in (2, 3):
+        pass_dn(2, hf)
+        pass_up(1, hf)
     for pr in range(PAIRS):
         got(a_x(pr))
         start(a_f(pr))
-    got(w_dn(2))
-    start(w_dn(3))
-    got(w_up(1))
-    start(w_up(2))
     for pr in range(PAIRS):
         got(a_s(pr), a_f(pr))
-    got(w_dn(3), w_up(2))
+    for hf in range(4):
+        got(w_dn(3, hf), w_up(2, hf))
 
     def ycopy(rb, way, n):
         return rc(tx.at[rb, way, n], rx.at[rb, way, n], ys.at[rb, way, n], yr.at[rb, way, n], yup if way == 0 else ydn)
@@ -243,14 +315,17 @@
         return rc(xtx.at[rb], xrx.at[rb], hs.at[rb], hr.at[rb], xhi)
 
     def ocopy(rb, dev_q, slot):
-        cols = pl.ds(pl.multiple_of(slot * C, C), C)
-        return rc(fin.at[rb], out_ref.at[:, cols], os.at[rb], orr.at[slot], (z * 4 + dev_q, head))
+        rows, cols = span(rb), pl.ds(pl.multiple_of(slot * C, C), C)
+        return rc(fin.at[rb], out_ref.at[rows, cols], os.at[rb], orr.at[slot, rb % 2], (z * 4 + dev_q, head))
+
+    def span(rb):
+        return pl.ds(pl.multiple_of((rb % 2) * H, H), H)
 
     def project(rb, yd, half):
         r = (((y + yd) % 4) * 2 + half + NZ - z) % NZ
         total = None
         for pr in range(PAIRS):
-            part = dot(a_all[rb, pr], w_all[r, pr * C:(pr + 1) * C, :])
+            part = dot(a_all[rb // 2, pr, span(rb), :], w_all[r, pr * C:(pr + 1) * C, :])
             total = part if total is None else total + part
         return total
 
@@ -287,29 +362,33 @@
         total = (keep[rb, 2 + xh] + xrx[rb].astype(F32)).astype(BF16)
         fin[rb] = total
 
-        @pl.when(rb != q)
+        @pl.when(rb // 2 != q)
         def _():
-            start(ocopy(rb, rb, q))
+            start(ocopy(rb, rb // 2, q))
 
     def rb_loop(t, carry):
         for lag, (stage) in enumerate((first_stage, second_stage, third_stage, fourth_stage)):
-            @pl.when((t >= lag) & (t < 4 + lag))
+            @pl.when((t >= lag) & (t < 8 + lag))
             def _():
                 stage(t - lag)
         return carry
 
-    lax.fori_loop(0, 7, rb_loop, 0)
-    out_ref[:, pl.ds(pl.multiple_of(q * C, C), C)] = fin[q]
-
-    for c in kv_z(0) + kv_z(1) + kv_z(2):
-        c.wait_send()
-    for dz in range(4):
-        for c in kv_x(dz) + kv_s(dz) + kv_f(dz):
-            c.wait_send()
-    for n in range(4):
-        w_dn(n).wait_send()
-    for n in range(3):
-        w_up(n).wait_send()
+    lax.fori_loop(0, 11, rb_loop, 0)
+    for n in range(2):
+        out_ref[n * H:(n + 1) * H, pl.ds(pl.multiple_of(q * C, C), C)] = fin[2 * q + n]
+
+    for i in range(2):
+        for dz in range(3):
+            kv_z(dz, i).wait_send()
+        for dz in range(4):
+            only(dz, low, high, lambda: kv_x(dz, i).wait_send())
+            only(dz, even, odd, lambda: kv_s(dz, i).wait_send())
+            only(dz, high, low, lambda: kv_f(dz, i).wait_send())
+    for hf in range(4):
+        for n in range(4):
+            w_dn(n, hf).wait_send()
+        for n in range(3):
+            w_up(n, hf).wait_send()
     for pr in range(PAIRS):
         for c in (a_x(pr), a_s(pr), a_f(pr)):
             c.wait_send()
@@ -320,14 +399,14 @@
                 ycopy(rb, way, n).wait_send()
         hcopy(rb).wait_send()
 
-        @pl.when(rb != q)
+        @pl.when(rb // 2 != q)
         def _():
-            ocopy(rb, rb, q).wait_send()
-            ocopy(rb, rb, rb).wait_recv()
+            ocopy(rb, rb // 2, q).wait_send()
+            ocopy(rb, rb // 2, rb // 2).wait_recv()
 
         return carry
 
-    lax.fori_loop(0, 4, finish, 0)
+    lax.fori_loop(0, 8, finish, 0)
 
 
 def body(queries, keys, values, windows, out_weight):
@@ -353,25 +432,25 @@
             pltpu.VMEM((3, 128, DH), BF16),
             pltpu.VMEM((3, VR, 128), BF16),
             pltpu.VMEM((3, 128, 128), F32),
-            pltpu.VMEM((4, 2, 3, T, C), BF16),
-            pltpu.VMEM((4, 2, 3, T, C), BF16),
-            pltpu.VMEM((4, 4, T, C), F32),
-            pltpu.VMEM((4, T, C), BF16),
-            pltpu.VMEM((4, T, C), BF16),
-            pltpu.VMEM((4, T, C), BF16),
+            pltpu.VMEM((8, 2, 3, H, C), BF16),
+            pltpu.VMEM((8, 2, 3, H, C), BF16),
+            pltpu.VMEM((8, 4, H, C), F32),
+            pltpu.VMEM((8, H, C), BF16),
+            pltpu.VMEM((8, H, C), BF16),
+            pltpu.VMEM((8, H, C), BF16),
             dma((2,)),
             dma((3, 2)), dma((3, 2)),
             dma((4, 2)), dma((4, 2)),
             dma((4, 2)), dma((4, 2)),
             dma((4, 2)), dma((4, 2)),
-            dma((4,)), dma((4,)),
-            dma((3,)), dma((3,)),
+            dma((4, 4)), dma((4, 4)),
+            dma((3, 4)), dma((3, 4)),
             dma((PAIRS,)), dma((PAIRS,)),
             dma((PAIRS,)), dma((PAIRS,)),
             dma((PAIRS,)), dma((PAIRS,)),
-            dma((4, 2, 3)), dma((4, 2, 3)),
-            dma((4,)), dma((4,)),
-            dma((4,)), dma((4,)),
+            dma((8, 2, 3)), dma((8, 2, 3)),
+            dma((8,)), dma((8,)),
+            dma((8,)), dma((4, 2)),
         ],
         compiler_params=pltpu.CompilerParams(
             collective_id=0, has_side_effects=True, vmem_limit_bytes=60 * 1024 * 1024),

time: 149 us -> 136 us (0.913)
  Pallas kernels: 146 us -> 133 us
    pallas_call x1, Pallas kernels: 146 us -> 133 us  [body(): pl.pallas_call(kernel, out_shape=jax.ShapeDtypeStruct((T, 4 * C), BF16),...]
where the time goes in v2:
time: 136 us
  Pallas kernels  133 us (98%)
  local copies, waits for them, and re-layouts  2.06 us (2%)
    pallas_call x1, Pallas kernels, body(): pl.pallas_call(kernel, out_shape=jax.ShapeDtypeStruct((T, 4 * C), BF16),...  133 us

profile of v2, /device:TPU:3, one launch (start us, length us, event | category | flops | bytes accessed | tf_op | source)
XLA Modules:
  0.0 136.0 jit_solution(16995651831606143221)
XLA Ops:
  0.7 133.3 %fused.1 = bf16[384,1024]{1,0:T(8,128)(2,1)} custom-call(bf16[384,1024]{1,0:T(8,128)(2,1)} %q_ref.1, bf16[384,128]{1,0:T(8,128)(2,1)} %k_ref.1, bf16[384,128]{1,0:T(8,128)(2,1)} %v_ref.1, s32[1]{0:T(128)S(6)} %copy.7.win_ref, bf16[1024,256]{1,0:T(8,128)(2,1)} %w_ref.1), custom_call_target="tpu_custom_call" | custom-call | tf_op jit(solution)/shard_map/fused/pallas_call | solution.py:416
  134.0 2.1 %copy.8 = bf16[384,1024]{1,0:T(8,128)(2,1)} copy(bf16[384,1024]{1,0:T(8,128)(2,1)} %fused.1) | data formatting | bytes 1572864

commit v3 on v2

--- a/solution.py
+++ b/solution.py
@@ -300,11 +300,6 @@
     for hf in (2, 3):
         pass_dn(2, hf)
         pass_up(1, hf)
-    for pr in range(PAIRS):
-        got(a_x(pr))
-        start(a_f(pr))
-    for pr in range(PAIRS):
-        got(a_s(pr), a_f(pr))
     for hf in range(4):
         got(w_dn(3, hf), w_up(2, hf))
 
@@ -366,11 +361,31 @@
         def _():
             start(ocopy(rb, rb // 2, q))
 
+    def chunk(t):
+        n = t // 2
+        return (((q // 2 + n // 2) % 2) * 2 + (q + n) % 2) * 2 + t % 2
+
     def rb_loop(t, carry):
-        for lag, (stage) in enumerate((first_stage, second_stage, third_stage, fourth_stage)):
+        @pl.when(t == 1)
+        def _():
+            for pr in range(PAIRS):
+                got(a_x(pr))
+                start(a_f(pr))
+
+        @pl.when(t == 2)
+        def _():
+            for pr in range(PAIRS):
+                got(a_s(pr))
+
+        @pl.when(t == 6)
+        def _():
+            for pr in range(PAIRS):
+                got(a_f(pr))
+
+        for lag, stage in enumerate((first_stage, second_stage, third_stage, fourth_stage)):
             @pl.when((t >= lag) & (t < 8 + lag))
             def _():
-                stage(t - lag)
+                stage(chunk(t - lag))
         return carry
 
     lax.fori_loop(0, 11, rb_loop, 0)

time: 136 us -> 131 us (0.963)
  Pallas kernels: 133 us -> 128 us
    pallas_call x1, Pallas kernels: 133 us -> 128 us  [body(): pl.pallas_call(kernel, out_shape=jax.ShapeDtypeStruct((T, 4 * C), BF16),...]
where the time goes in v3:
time: 131 us; the launch traced here: 130 us
  Pallas kernels  128 us (98%)
  local copies, waits for them, and re-layouts  2.06 us (2%)
    pallas_call x1, Pallas kernels, body(): pl.pallas_call(kernel, out_shape=jax.ShapeDtypeStruct((T, 4 * C), BF16),...  128 us

profile of v3, /device:TPU:3, one launch (start us, length us, event | category | flops | bytes accessed | tf_op | source)
XLA Modules:
  0.0 130.3 jit_solution(6680582508009128710)
XLA Ops:
  0.7 127.6 %fused.1 = bf16[384,1024]{1,0:T(8,128)(2,1)} custom-call(bf16[384,1024]{1,0:T(8,128)(2,1)} %q_ref.1, bf16[384,128]{1,0:T(8,128)(2,1)} %k_ref.1, bf16[384,128]{1,0:T(8,128)(2,1)} %v_ref.1, s32[1]{0:T(128)S(6)} %copy.7.win_ref, bf16[1024,256]{1,0:T(8,128)(2,1)} %w_ref.1), custom_call_target="tpu_custom_call" | custom-call | tf_op jit(solution)/shard_map/fused/pallas_call | solution.py:431
  128.3 2.1 %copy.8 = bf16[384,1024]{1,0:T(8,128)(2,1)} copy(bf16[384,1024]{1,0:T(8,128)(2,1)} %fused.1) | data formatting | bytes 1572864
